TPU v7x, 256 devices: a whole 4x4x8 slice. The times are simulated.
256 devices in a mesh: row: 4 (over z_hi, core), col: 64 (over x, y, z_lo).
Axes of the slice: x: 4, y: 4, z: 8 (z_hi: 2, z_lo: 4; z = z_hi * 4 + z_lo), core: 2. Of those that a mesh axis runs over, the one named last changes fastest.
Arguments:
- pre_act: bfloat16 [24576, 4096], P('col'), may hold values from -16 to 16
- grad_out: bfloat16 [24576, 4096], P('col', 'row'), may hold values from -6 to 6
- w_down: bfloat16 [4096, 4096], P('col', 'row'), may hold values from -0.09375 to 0.09375
Outputs:
- w_grad: float32 [4096, 4096], P('col', 'row')
- grad_pre: bfloat16 [24576, 4096], P('col', 'row')
All inputs are finite; a program needn't handle non-finite values.
Results may differ from a plain program's by a relative error of at most 0.0095.
Values may be sent and summed in bfloat16 or wider, within the bound.
A program may use at most 128 MiB of HBM per device.

v0:
```python
import jax
import jax.numpy as jnp
from jax import lax
from jax.sharding import Mesh
from jax.sharding import PartitionSpec as P

COL = ("col_0", "col_1", "col_2")


def summed_rows(subtotal, axes):
    for axis in axes:
        subtotal = lax.psum_scatter(subtotal, axis, scatter_dimension=0, tiled=True)
    return subtotal


def per_device(pre_act, grad_out, w_down):
    hidden = jnp.maximum(pre_act, jnp.zeros((), jnp.bfloat16))
    col_count = lax.axis_size(COL)
    row_count = lax.axis_size("row")
    scale = 1.0 / jnp.sqrt(jnp.float32(hidden.shape[0] * col_count))
    quarter = hidden.shape[1] // row_count
    partial_sum = lax.dot_general(
        grad_out,
        lax.all_gather(w_down, COL, axis=0, tiled=True),
        (((1,), (1,)), ((), ())),
        preferred_element_type=jnp.float32,
    )
    term = lax.dot_general(
        hidden, grad_out, (((0,), (0,)), ((), ())), preferred_element_type=jnp.float32
    )
    w_grad = summed_rows(term * scale, COL)
    own_sum = lax.psum_scatter(
        partial_sum.astype(jnp.bfloat16), "row", scatter_dimension=1, tiled=True
    ).astype(jnp.float32)
    offset_pre = lax.axis_index("row") * quarter
    own_pre = lax.dynamic_slice_in_dim(pre_act, offset_pre, quarter, 1)
    grad_pre = jnp.where(own_pre > 0, own_sum, jnp.zeros((), jnp.float32)).astype(jnp.bfloat16)
    return (w_grad, grad_pre)


def solution(mesh):
    torus = Mesh(
        mesh.devices.reshape(mesh.shape["row"], 4, 4, 4), ("row", "col_0", "col_1", "col_2")
    )
    placed = (P(COL, None), P(COL, "row"), P(COL, "row"))
    return jax.shard_map(
        per_device,
        mesh=torus,
        in_specs=placed,
        out_specs=(P(COL, "row"), P(COL, "row")),
        check_vma=False,
    )
```

profile of v0, /device:TPU:1, one launch (start us, length us, event | category | flops | bytes accessed | tf_op | source)
XLA Modules:
  0.0 517.6 jit_solution(3365251138714423770)
XLA Ops:
  8.0 0.0 copy-start
  8.0 0.0 reduce-scatter.5.cloned.1.call-start
  8.1 1.1 copy-done
  9.1 10.0 %convolution_multiply_fusion = f32[4096,1024]{1,0:T(8,128)} fusion(bf16[384,1024]{1,0:T(8,128)(2,1)S(1)} %copy-done, bf16[384,4096]{1,0:T(8,128)(2,1)} %param.3), kind=kOutput, calls=%fused_computation | convolution fusion | flops 3226992640 | bytes 20709376 | tf_op jit(solution)/shard_map/dot_general | solution.py:28
  19.2 0.0 reduce-scatter.5.cloned.1.call-update
  19.2 0.0 all-gather.2.cloned.1.call-start
  19.2 0.5 all-gather.2.cloned.1.call-update
  19.8 0.0 reduce-scatter.7.cloned.1.call-start
  19.8 153.7 %reduce-scatter.5.cloned.1.call-done = f32[1024,1024]{1,0:T(8,128)} async-done(((f32[4096,1024]{1,0:T(8,128)}), f32[1024,1024]{1,0:T(8,128)}) %reduce-scatter.5.cloned.1.call-update) | async-done | bytes 4194320 | tf_op jit(solution)/shard_map/reduce_scatter | solution.py:12
  173.5 0.0 reduce-scatter.7.cloned.1.call-update
  173.6 0.0 reduce-scatter.11.cloned.1.call-start
  173.6 186.3 %all-gather.2.cloned.1.call-done = bf16[4096,1024]{1,0:T(8,128)(2,1)} async-done(((bf16[64,1024]{1,0:T(8,128)(2,1)}), bf16[4096,1024]{1,0:T(8,128)(2,1)}) %all-gather.2.cloned.1.call-update) | async-done | bytes 8388624 | tf_op jit(solution)/shard_map/all_gather | solution.py:24
  359.9 10.3 %convolution_convert_fusion = bf16[384,4096]{1,0:T(8,128)(2,1)} fusion(bf16[384,1024]{1,0:T(8,128)(2,1)S(1)} %copy-done, bf16[4096,1024]{1,0:T(8,128)(2,1)} %all-gather.2.cloned.1.call-done), kind=kOutput, calls=%fused_computation.1 | convolution fusion | flops 3222798336 | bytes 12320768 | tf_op jit(solution)/shard_map/dot_general | solution.py:22
  370.3 0.0 reduce-scatter.11.cloned.1.call-update
  370.3 0.0 reduce-scatter.9.cloned.1.call-start
  370.3 0.0 reduce-scatter.7.cloned.1.call-done
  370.4 0.5 reduce-scatter.9.cloned.1.call-update
  370.9 108.1 %reduce-scatter.11.cloned.1.call-done = bf16[384,1024]{1,0:T(8,128)(2,1)} async-done(((bf16[384,4096]{1,0:T(8,128)(2,1)}), bf16[384,1024]{1,0:T(8,128)(2,1)}) %reduce-scatter.11.cloned.1.call-update) | async-done | bytes 786448 | tf_op jit(solution)/shard_map/reduce_scatter | solution.py:32
  479.0 2.5 select_convert_fusion
  481.5 28.9 %reduce-scatter.9.cloned.1.call-done = f32[64,1024]{1,0:T(8,128)} async-done(((f32[256,1024]{1,0:T(8,128)}), f32[64,1024]{1,0:T(8,128)}) %reduce-scatter.9.cloned.1.call-update) | async-done | bytes 262160 | tf_op jit(solution)/shard_map/reduce_scatter | solution.py:12
Async XLA Ops:
  8.0 1.1 copy-start
  8.0 165.5 %reduce-scatter.5.cloned.1.call-start = ((), (), s32[]{:S(2)}) async-start(), calls=%async_computation.4 | async-start | bytes 20971520 | tf_op jit(solution)/shard_map/reduce_scatter | solution.py:12
  19.2 340.7 %all-gather.2.cloned.1.call-start = ((), (), s32[]{:S(2)}) async-start(), calls=%async_computation.7 | async-start | bytes 8519680 | tf_op jit(solution)/shard_map/all_gather | solution.py:24
  19.8 350.6 %reduce-scatter.7.cloned.1.call-start = ((), (), s32[]{:S(2)}) async-start(), calls=%async_computation.5 | async-start | bytes 5242880 | tf_op jit(solution)/shard_map/reduce_scatter | solution.py:12
  173.6 305.4 %reduce-scatter.11.cloned.1.call-start = ((), (), s32[]{:S(2)}) async-start(), calls=%async_computation.8 | async-start | bytes 3932160 | tf_op jit(solution)/shard_map/reduce_scatter | solution.py:32
  370.3 140.2 %reduce-scatter.9.cloned.1.call-start = ((), (), s32[]{:S(2)}) async-start(), calls=%async_computation.6 | async-start | bytes 1310720 | tf_op jit(solution)/shard_map/reduce_scatter | solution.py:12
Sparse Core Ops, SparseCore 0:
  19.3 154.1 reduce-scatter.4
  176.1 113.8 reduce-scatter.6
  370.4 108.5 reduce-scatter.10
  482.0 28.4 reduce-scatter.8
Sparse Core Ops, SparseCore 1:
  21.5 338.4 all-gather.1
where the time goes:
time: 518 us
  waiting for transfers between devices  478 us (92%)
  matrix products  20.4 us (4%)
  between operations  15.2 us (3%)
    all_gather x1, waiting for transfers between devices, per_device(): lax.all_gather(w_down, COL, axis=0, tiled=True)  186 us
    reduce_scatter x3, waiting for transfers between devices, summed_rows(): subtotal = lax.psum_scatter(subtotal, axis, scatter_dimension=0, tiled=True)  183 us
    reduce_scatter x1, waiting for transfers between devices, per_device(): lax.psum_scatter(partial_sum.astype(jnp.bfloat16), 'row', scatter_dimensi...  108 us
  transfers between devices with their start and end apart: 5, of which 4 were waited for; matrix products, arithmetic and copies ran while one was open for 2% of the time, Pallas kernels for 0%

commit v1 on v0

v1 whole, which is shorter than its diff:
```python
import jax
import jax.numpy as jnp
from jax import lax
from jax.experimental import pallas as pl
from jax.experimental.pallas import tpu as pltpu
from jax.sharding import Mesh
from jax.sharding import PartitionSpec as P

AXES = ("zh", "cc", "x", "y", "zl")
COL = ("x", "y", "zl")
ROW = ("zh", "cc")
MESH = pl.DeviceIdType.MESH
BF = jnp.bfloat16
F32 = jnp.float32


def body(
    pre, go, wd, wout, gout,
    a_all, p_all, w_all, pt, acc, o_keep, o_give, o_take, keep, c_give, c_take, c_send, c_in, z_in,
    g_send, g_recv, g_sum, gz_send, gz_recv,
    wz_s, wz_r, wy_s, wy_r, a_s, a_r, p_s, p_r, q_s, q_r, d_s, d_r, c_s, c_r,
    z_s, z_r, g_s, g_r, h_s, h_r,
):
    zh, cc, x, y, zl = [lax.axis_index(name) for name in AXES]
    t, q = go.shape
    half = t // 2
    u = wd.shape[0]
    v = 4 * u
    scale = 1.0 / jnp.sqrt(jnp.float32(t * 64))

    def dev(dx=0, dy=0, dz=0, core=None, other=False):
        return (
            1 - zh if other else zh,
            cc if core is None else core,
            lax.rem(x + dx, 4),
            lax.rem(y + dy, 4),
            lax.rem(zl + dz, 4),
        )

    def copy(src, dst, ss, rs, to):
        return pltpu.make_async_remote_copy(
            src_ref=src, dst_ref=dst, send_sem=ss, recv_sem=rs, device_id=to, device_id_type=MESH
        )

    twin = 1 - cc
    lead = lax.rem(x, 2)
    peers = [dev(core=twin), dev(other=True)]
    peers += [dev(dx=d, core=c) for d in (1, 2, 3) for c in (cc, twin)]
    peers += [dev(dy=d) for d in (1, 2, 3)] + [dev(dz=d) for d in (1, 2, 3)]
    barrier = pltpu.get_barrier_semaphore()
    for peer in peers:
        pl.semaphore_signal(barrier, inc=1, device_id=peer, device_id_type=MESH)
    pl.semaphore_wait(barrier, len(peers))

    sent = []

    def send(c):
        c.start()
        sent.append(c)

    def w_rows(yy, zz):
        return pl.ds(pl.multiple_of(v * yy + u * zz, u), u)

    here = w_rows(y, zl)
    for d in (1, 2, 3):
        send(copy(wd, w_all.at[here], wz_s.at[d - 1], wz_r.at[d - 1], dev(dz=d)))
    for d in (1, 2, 3):
        send(copy(wd, w_all.at[here], wy_s.at[d - 1, 0], wy_r.at[d - 1, 0], dev(dy=d)))

    def a_half(slot, h):
        return a_all.at[pl.ds(t * slot + half * h, half)]

    for h in (0, 1):
        send(copy(go.at[pl.ds(half * h, half)], a_half(1, h), a_s.at[0, h], a_r.at[0, h], dev(dx=1)))
        g = 1 - h
        send(copy(go.at[pl.ds(half * g, half)], a_half(2, g), a_s.at[1, g], a_r.at[1, g], dev(dx=3)))

    a_all[0:t] = go[...]
    w_all[here] = wd[...]

    def p_cols(dx, k):
        block = q * lax.rem(x + dx, 4) + v * lax.rem(y + 1 + k, 4)
        return pl.ds(pl.multiple_of(block, v), v)

    for k in range(4):
        p_all[k, 0:t] = pre[:, p_cols(0, k)]

    for d in (1, 2, 3):
        rows = w_rows(y, lax.rem(zl + 4 - d, 4))
        copy(wd, w_all.at[rows], wz_s.at[d - 1], wz_r.at[d - 1], dev(dz=d)).wait_recv()
        for e in (1, 2, 3):
            send(copy(w_all.at[rows], w_all.at[rows], wy_s.at[e - 1, d], wy_r.at[e - 1, d], dev(dy=e)))

    def a_wait(slot, h):
        copy(a_half(slot, h), a_half(slot, h), a_s.at[slot - 1, h], a_r.at[slot - 1, h], dev(dx=1)).wait_recv()

    a_wait(1, 0)
    send(copy(a_half(1, 0), a_half(3, 0), a_s.at[2, 0], a_r.at[2, 0], dev(dx=1)))
    a_wait(2, 1)
    send(copy(a_half(2, 1), a_half(3, 1), a_s.at[2, 1], a_r.at[2, 1], dev(dx=3)))

    for e in (1, 2, 3):
        for d in range(4):
            rows = w_rows(lax.rem(y + 4 - e, 4), lax.rem(zl + 4 - d, 4))
            copy(wd, w_all.at[rows], wy_s.at[e - 1, d], wy_r.at[e - 1, d], dev(dy=e)).wait_recv()

    mine = pl.ds(pl.multiple_of(half * cc, half), half)
    theirs = pl.ds(pl.multiple_of(half * twin, half), half)

    def partial(slot, out):
        @pl.loop(0, 4)
        def _(n):
            cols = pl.ds(pl.multiple_of(n * v, v), v)
            out[:, cols] = lax.dot_general(
                a_all[t * slot:t * slot + t], w_all[cols, :], (((1,), (1,)), ((), ())),
                preferred_element_type=F32,
            )

    def swap(slot):
        return copy(c_give.at[slot - 1], c_take.at[slot - 1], d_s.at[slot], d_r.at[slot], dev(core=twin))

    def offer(slot):
        partial(slot, acc)
        c_give[slot - 1] = acc[theirs].astype(BF)
        keep[slot - 1] = acc[mine]
        send(swap(slot))

    def deliver(slot, dx):
        swap(slot).wait_recv()
        c_send[slot - 1] = (keep[slot - 1] + c_take[slot - 1].astype(F32)).astype(BF)
        target = c_in.at[lax.div(x, 2), mine]
        send(copy(c_send.at[slot - 1], target, c_s.at[slot - 1], c_r.at[lax.div(x, 2), cc], dev(dx=dx, core=lead)))

    def arrived(i, h):
        rows = c_in.at[i, pl.ds(half * h, half)]
        copy(rows, rows, c_s.at[0], c_r.at[i, h], dev(dx=1)).wait_recv()

    def across(h):
        rows = pl.ds(half * h, half)
        return copy(c_in.at[1 - zh, rows], z_in.at[rows], z_s.at[h], z_r.at[h], dev(other=True))

    far = lax.rem(2 * (1 - zh) + cc + 4 - x, 4)

    def onward():
        for h in (0, 1):
            arrived(1 - zh, h)
            across(h).start()

    partial(0, o_keep)
    own = copy(o_give, o_take, d_s.at[0], d_r.at[0], dev(core=twin))

    @pl.when(cc != lead)
    def _():
        o_give[...] = o_keep[...].astype(BF)
        own.start()

    a_wait(1, 1)
    offer(1)

    @pl.when(cc == lead)
    def _():
        own.wait_recv()
        c_in[lax.div(x, 2)] = (o_keep[...] + o_take[...].astype(F32)).astype(BF)

        @pl.when(far == 0)
        def _():
            for h in (0, 1):
                across(h).start()

    a_wait(2, 0)
    offer(2)
    deliver(1, 3)
    deliver(2, 1)
    a_wait(3, 0)
    a_wait(3, 1)
    offer(3)

    def p_copy(slot, k):
        dx = (1, 3, 2)[slot - 1]
        rows = pl.ds(pl.multiple_of(t * slot + half * cc, half), half)
        return copy(
            pre.at[mine, p_cols(dx, k)], p_all.at[k, rows], p_s.at[slot - 1, k], p_r.at[slot - 1, k], dev(dx=dx)
        )

    def q_copy(slot, k):
        rows = p_all.at[k, pl.ds(pl.multiple_of(t * slot + half * cc, half), half)]
        return copy(rows, rows, q_s.at[slot - 1, k], q_r.at[slot - 1, k], dev(core=twin))

    for k in range(4):
        for slot in (1, 2, 3):
            send(p_copy(slot, k))
    deliver(3, 2)

    @pl.when((far == 1) | (far == 3))
    def _():
        onward()

    def g_copy(k):
        return copy(g_send.at[k], g_recv.at[k], g_s.at[k], g_r.at[k], dev(dy=1 + k))

    for k in range(4):
        for slot in (1, 2, 3):
            p_copy(slot, k).wait_recv()
            send(q_copy(slot, k))
        for slot in (1, 2, 3):
            q_copy(slot, k).wait_recv()
        pt[...] = jnp.maximum(p_all[k], jnp.zeros((), BF)).T

        @pl.loop(0, 4)
        def _(n):
            cols = pl.ds(pl.multiple_of(n * v, v), v)
            part = jnp.dot(pt[...], a_all[:, cols], preferred_element_type=F32)
            if k < 3:
                g_send[k, :, cols] = part.astype(BF)
            else:
                g_sum[:, cols] = part

        if k < 3:
            send(g_copy(k))

    @pl.when(far == 2)
    def _():
        onward()

    for k in range(3):
        g_copy(k).wait_recv()
    g_sum[...] += g_recv[0].astype(F32) + g_recv[1].astype(F32) + g_recv[2].astype(F32)

    def h_copy(d):
        return copy(gz_send.at[d - 1], gz_recv.at[d - 1], h_s.at[d - 1], h_r.at[d - 1], dev(dz=d))

    for d in (1, 2, 3):
        gz_send[d - 1] = g_sum[pl.ds(pl.multiple_of(u * lax.rem(zl + d, 4), u), u)].astype(BF)
        send(h_copy(d))
    for d in (1, 2, 3):
        h_copy(d).wait_recv()
    total = g_sum[pl.ds(pl.multiple_of(u * zl, u), u)]
    total += gz_recv[0].astype(F32) + gz_recv[1].astype(F32) + gz_recv[2].astype(F32)
    wout[...] = total * scale

    @pl.when(x != 2 * zh + cc)
    def _():
        for h in (0, 1):
            arrived(zh, h)

    for h in (0, 1):
        across(h).wait_recv()
    own_pre = pre[:, pl.ds(pl.multiple_of(q * (2 * zh + cc), q), q)]
    both = c_in[zh].astype(F32) + z_in[...].astype(F32)
    gout[...] = jnp.where(own_pre.astype(F32) > 0, both, 0.0).astype(BF)

    for c in sent:
        c.wait_send()
    for h in (0, 1):
        across(h).wait_send()

    @pl.when(cc != lead)
    def _():
        own.wait_send()


def per_device(pre_act, grad_out, w_down):
    t, q = grad_out.shape
    u = w_down.shape[0]
    v = 4 * u
    half = t // 2
    vm = pltpu.VMEM
    sem = lambda *n: pltpu.SemaphoreType.DMA(n)
    space = pl.BlockSpec(memory_space=pltpu.VMEM)
    return pl.pallas_call(
        body,
        out_shape=(jax.ShapeDtypeStruct((u, q), F32), jax.ShapeDtypeStruct((t, q), BF)),
        in_specs=[space] * 3,
        out_specs=(space, space),
        scratch_shapes=[
            vm((4 * t, q), BF), vm((4, 4 * t, v), BF), vm((4 * v, q), BF), vm((v, 4 * t), BF),
            vm((t, q), F32), vm((t, q), F32), vm((t, q), BF), vm((t, q), BF),
            vm((3, half, q), F32), vm((3, half, q), BF), vm((3, half, q), BF), vm((3, half, q), BF),
            vm((2, t, q), BF), vm((t, q), BF),
            vm((3, v, q), BF), vm((3, v, q), BF), vm((v, q), F32), vm((3, u, q), BF), vm((3, u, q), BF),
            sem(3), sem(3), sem(3, 4), sem(3, 4), sem(3, 2), sem(3, 2), sem(3, 4), sem(3, 4), sem(3, 4), sem(3, 4),
            sem(4), sem(4), sem(3), sem(2, 2),
            sem(2), sem(2), sem(3), sem(3), sem(3), sem(3),
        ],
        compiler_params=pltpu.CompilerParams(
            collective_id=0, has_side_effects=True, vmem_limit_bytes=60 * 2**20
        ),
        name="backward",
    )(pre_act, grad_out, w_down)


def solution(mesh):
    torus = Mesh(mesh.devices.reshape(2, mesh.shape["row"] // 2, 4, 4, 4), AXES)
    return jax.shard_map(
        per_device,
        mesh=torus,
        in_specs=(P(COL, None), P(COL, ROW), P(COL, ROW)),
        out_specs=(P(COL, ROW), P(COL, ROW)),
        check_vma=False,
    )
```

time: 518 us -> 115 us (0.22)
  the two profiles are of different devices: /device:TPU:1 before, /device:TPU:37 now
where the time goes in v1:
time: 115 us
  Pallas kernels  111 us (97%)
  local copies, waits for them, and re-layouts  3.73 us (3%)
    pallas_call x1, Pallas kernels, per_device(): pl.pallas_call(body, out_shape=(jax.ShapeDtypeStruct((u, q), F32), jax.Sh...  111 us
    unnamed x2, local copies, waits for them, and re-layouts  3.73 us

profile of v1, /device:TPU:37, one launch (start us, length us, event | category | flops | bytes accessed | tf_op | source)
XLA Modules:
  0.0 115.3 jit_solution(14944341490120076884)
XLA Ops:
  0.6 111.0 %backward.1 = (f32[64,1024]{1,0:T(8,128)}, bf16[384,1024]{1,0:T(8,128)(2,1)}) custom-call(bf16[384,4096]{1,0:T(8,128)(2,1)} %pre.1, bf16[384,1024]{1,0:T(8,128)(2,1)} %go.1, bf16[64,1024]{1,0:T(8,128)(2,1)} %wd.1), custom_call_target="tpu_custom_call" | custom-call | tf_op jit(solution)/shard_map/backward/pallas_call | solution.py:270
  111.6 1.7 %copy.7 = f32[64,1024]{1,0:T(8,128)} copy(f32[64,1024]{1,0:T(8,128)} %get-tuple-element.4) | data formatting | bytes 524288
  113.3 2.1 %copy.8 = bf16[384,1024]{1,0:T(8,128)(2,1)} copy(bf16[384,1024]{1,0:T(8,128)(2,1)} %get-tuple-element.5) | data formatting | bytes 1572864

commit v2 on v0

v2 whole, which is shorter than its diff:
```python
import jax
import jax.numpy as jnp
from jax import lax
from jax.experimental import pallas as pl
from jax.experimental.pallas import tpu as pltpu
from jax.sharding import Mesh
from jax.sharding import PartitionSpec as P

AXES = ("zh", "cc", "x", "y", "zl")
COL = ("x", "y", "zl")
ROW = ("zh", "cc")
MESH = pl.DeviceIdType.MESH
BF = jnp.bfloat16
F32 = jnp.float32
TURNS = (1, 3, 2, 0)
FROM = (0, 1, 3, 2)


def body(
    pre_h, go_h, wd_h, wout, gout,
    pre, a_all, p_all, w_all, pt, acc, o_keep, o_give, o_take, keep, c_give, c_take, c_send, c_in, z_in,
    g_send, g_recv, g_sum, gz_send, gz_recv,
    l_s, wz_s, wz_r, wy_s, wy_r, a_s, a_r, p_s, p_r, q_s, q_r, o_s, o_r, d_s, d_r, c_s, c_r,
    z_s, z_r, g_s, g_r, h_s, h_r,
):
    zh, cc, x, y, zl = [lax.axis_index(name) for name in AXES]
    t, q = go_h.shape
    half = t // 2
    u = wd_h.shape[0]
    v = 4 * u
    scale = 1.0 / jnp.sqrt(jnp.float32(t * 64))

    def dev(dx=0, dy=0, dz=0, core=None, other=False):
        return (
            1 - zh if other else zh,
            cc if core is None else core,
            lax.rem(x + dx, 4),
            lax.rem(y + dy, 4),
            lax.rem(zl + dz, 4),
        )

    def copy(src, dst, ss, rs, to):
        return pltpu.make_async_remote_copy(
            src_ref=src, dst_ref=dst, send_sem=ss, recv_sem=rs, device_id=to, device_id_type=MESH
        )

    def w_rows(yy, zz):
        return pl.ds(pl.multiple_of(v * yy + u * zz, u), u)

    def w_block(dy, d):
        return w_all.at[w_rows(lax.rem(y + 4 - dy, 4), lax.rem(zl + 4 - d, 4))]

    def p_cols(dx, k):
        block = q * lax.rem(x + dx, 4) + v * lax.rem(y + TURNS[k], 4)
        return pl.ds(pl.multiple_of(block, v), v)

    twin = 1 - cc
    lead = lax.rem(x, 2)
    peers = [dev(core=twin), dev(other=True)]
    peers += [dev(dx=d, core=c) for d in (1, 2, 3) for c in (cc, twin)]
    peers += [dev(dy=d) for d in (1, 2, 3)] + [dev(dz=d) for d in (1, 2, 3)]
    with jax.named_scope("s00_barrier"):
        barrier = pltpu.get_barrier_semaphore()
        for peer in peers:
            pl.semaphore_signal(barrier, inc=1, device_id=peer, device_id_type=MESH)

    load_w = pltpu.make_async_copy(wd_h, w_block(0, 0), l_s.at[0])
    load_a = pltpu.make_async_copy(go_h, a_all.at[0:t], l_s.at[1])
    load_p = pltpu.make_async_copy(pre_h, pre, l_s.at[2])
    loads = [load_w, load_a, load_p]
    for c in loads:
        c.start()
    with jax.named_scope("s01_loads"):
        load_w.wait()
        load_a.wait()
    with jax.named_scope("s02_barrier"):
        pl.semaphore_wait(barrier, len(peers))

    sent = []

    def send(c):
        c.start()
        sent.append(c)

    def wz(d):
        return copy(w_block(0, 0), w_block(0, 0), wz_s.at[d - 1], wz_r.at[d - 1], dev(dz=d))

    def wy(e, d):
        block = (w_block(0, d), w_block(0, d), w_block(1, d) if d % 2 == 0 else w_block(3, d))[e]
        dy = (1, 3, 1 if d % 2 == 0 else 3)[e]
        return copy(block, block, wy_s.at[e, d], wy_r.at[e, d], dev(dy=dy))

    def wy_wait(e, d):
        block = w_block((1, 3, 2)[e], d)
        copy(block, block, wy_s.at[e, d], wy_r.at[e, d], dev(dy=1)).wait_recv()

    def a_half(slot, h):
        return a_all.at[pl.ds(t * slot + half * h, half)]

    for d in (1, 2, 3):
        send(wz(d))
    send(wy(0, 0))
    send(wy(1, 0))
    for h in (0, 1):
        send(copy(a_half(0, h), a_half(1, h), a_s.at[0, h], a_r.at[0, h], dev(dx=1)))
        g = 1 - h
        send(copy(a_half(0, g), a_half(2, g), a_s.at[1, g], a_r.at[1, g], dev(dx=3)))

    mine = pl.ds(pl.multiple_of(half * cc, half), half)
    theirs = pl.ds(pl.multiple_of(half * twin, half), half)

    def p_copy(slot, k):
        dx = (1, 3, 2)[slot - 1]
        rows = pl.ds(pl.multiple_of(t * slot + half * cc, half), half)
        return copy(
            pre.at[mine, p_cols(dx, k)], p_all.at[k, rows], p_s.at[slot - 1, k], p_r.at[slot - 1, k], dev(dx=dx)
        )

    def q_copy(slot, k):
        rows = p_all.at[k, pl.ds(pl.multiple_of(t * slot + half * cc, half), half)]
        return copy(rows, rows, q_s.at[slot - 1, k], q_r.at[slot - 1, k], dev(core=twin))

    def p_send(k):
        for slot in (1, 2, 3):
            send(p_copy(slot, k))

    load_p.wait()
    p_send(0)

    with jax.named_scope("s03_local"):
        for k in range(4):
            p_all[k, 0:t] = pre[:, p_cols(0, k)]

    def a_wait(slot, h):
        copy(a_half(slot, h), a_half(slot, h), a_s.at[slot - 1, h], a_r.at[slot - 1, h], dev(dx=1)).wait_recv()

    def a_relay():
        a_wait(1, 0)
        send(copy(a_half(1, 0), a_half(3, 0), a_s.at[2, 0], a_r.at[2, 0], dev(dx=1)))
        a_wait(2, 1)
        send(copy(a_half(2, 1), a_half(3, 1), a_s.at[2, 1], a_r.at[2, 1], dev(dx=3)))

    for d in (1, 2, 3):
        with jax.named_scope("s04_wz"):
            block = w_block(0, d)
            copy(block, block, wz_s.at[d - 1], wz_r.at[d - 1], dev(dz=d)).wait_recv()
            send(wy(0, d))
            send(wy(1, d))
        with jax.named_scope("s05_wy"):
            wy_wait((d - 1) % 2, d - 1)
            send(wy(2, d - 1))
        if d == 2:
            with jax.named_scope("s05_arelay"):
                a_relay()
    with jax.named_scope("s05_wy"):
        wy_wait(1, 3)
        send(wy(2, 3))

    def w_cols(n):
        return pl.ds(pl.multiple_of(v * lax.rem(y + 4 - FROM[n], 4), v), v)

    def partial(slot, n, out):
        out[...] = lax.dot_general(
            a_all[t * slot:t * slot + t], w_all[w_cols(n), :], (((1,), (1,)), ((), ())),
            preferred_element_type=F32,
        )

    def swap(slot, n):
        i = slot - 1
        return copy(c_give.at[i, n], c_take.at[i, n], d_s.at[i, n], d_r.at[i, n], dev(core=twin))

    def offer(slot, n):
        partial(slot, n, acc)
        c_give[slot - 1, n] = acc[theirs].astype(BF)
        keep[slot - 1, n] = acc[mine]
        send(swap(slot, n))

    def deliver(slot, n):
        i = slot - 1
        swap(slot, n).wait_recv()
        c_send[i, n] = (keep[i, n] + c_take[i, n].astype(F32)).astype(BF)
        target = c_in.at[lax.div(x, 2), n, mine]
        to = dev(dx=(3, 1, 2)[i], core=lead)
        send(copy(c_send.at[i, n], target, c_s.at[i, n], c_r.at[lax.div(x, 2), n, cc], to))

    def arrived(i, n):
        for h in (0, 1):
            rows = c_in.at[i, n, pl.ds(half * h, half)]
            copy(rows, rows, c_s.at[0, 0], c_r.at[i, n, h], dev(dx=1)).wait_recv()

    def across(n):
        return copy(c_in.at[1 - zh, n], z_in.at[n], z_s.at[n], z_r.at[n], dev(other=True))

    far = lax.rem(2 * (1 - zh) + cc + 4 - x, 4)

    def onward():
        for n in range(4):
            arrived(1 - zh, n)
            across(n).start()

    with jax.named_scope("s06_a12"):
        a_wait(1, 1)
        a_wait(2, 0)
    for n in range(4):
        with jax.named_scope("s07_wy"):
            if n in (1, 2):
                for d in range(4):
                    if d % 2 == n % 2:
                        wy_wait(n - 1, d)
            if n == 3:
                for d in range(4):
                    wy_wait(2, d)
        with jax.named_scope("s08_offer12"):
            offer(1, n)
            offer(2, n)
            if n > 0:
                deliver(1, n - 1)
                deliver(2, n - 1)
    with jax.named_scope("s08_deliver12"):
        deliver(1, 3)
        deliver(2, 3)

    own = copy(o_give, o_take, o_s.at[0], o_r.at[0], dev(core=twin))
    with jax.named_scope("s09_own"):
        for n in range(4):
            partial(0, n, o_keep.at[n])

        @pl.when(cc != lead)
        def _():
            o_give[...] = o_keep[...].astype(BF)
            own.start()

    with jax.named_scope("s10_a3"):
        a_wait(3, 0)
        a_wait(3, 1)
    with jax.named_scope("s10_offer3"):
        for n in range(4):
            offer(3, n)

    with jax.named_scope("s11_own"):

        @pl.when(cc == lead)
        def _():
            own.wait_recv()
            c_in[lax.div(x, 2)] = (o_keep[...] + o_take[...].astype(F32)).astype(BF)

            @pl.when(far == 0)
            def _():
                for n in range(4):
                    across(n).start()

    def onward3(n):
        @pl.when(far == 2)
        def _():
            arrived(1 - zh, n)
            across(n).start()

    with jax.named_scope("s12_deliver3"):
        p_send(1)
        deliver(3, 0)
        p_send(2)
        deliver(3, 1)
        deliver(3, 2)
        p_send(3)
        deliver(3, 3)

    with jax.named_scope("s13_onward1"):

        @pl.when((far == 1) | (far == 3))
        def _():
            onward()

    def g_copy(k, w):
        return copy(g_send.at[k, w], g_recv.at[k, w], g_s.at[k, w], g_r.at[k, w], dev(dy=TURNS[k]))

    def weight_part(k):
        with jax.named_scope("s14_pwait"):
            for slot in (1, 2, 3):
                p_copy(slot, k).wait_recv()
                send(q_copy(slot, k))
        with jax.named_scope("s15_qwait"):
            for slot in (1, 2, 3):
                q_copy(slot, k).wait_recv()
        with jax.named_scope("s16_g"):
            pt[...] = jnp.maximum(p_all[k], jnp.zeros((), BF)).T

            for w in (0, 1):

                @pl.loop(0, 2)
                def _(n):
                    cols = pl.ds(pl.multiple_of(n * v, v), v)
                    from_cols = pl.ds(pl.multiple_of((2 * w + n) * v, v), v)
                    part = jnp.dot(pt[...], a_all[:, from_cols], preferred_element_type=F32)
                    if k < 3:
                        g_send[k, w, :, cols] = part.astype(BF)
                    else:
                        g_sum[w, :, cols] = part

                if k < 3:
                    send(g_copy(k, w))

    weight_part(0)
    weight_part(1)
    with jax.named_scope("s17_onward3"):
        onward3(0)
    weight_part(2)
    with jax.named_scope("s17_onward3"):
        onward3(1)
        onward3(2)
    weight_part(3)

    def h_copy(w, d):
        return copy(gz_send.at[w, d - 1], gz_recv.at[w, d - 1], h_s.at[w, d - 1], h_r.at[w, d - 1], dev(dz=d))

    def over_y(w):
        with jax.named_scope("s20_gwait"):
            for k in range(3):
                g_copy(k, w).wait_recv()
        g_sum[w] += g_recv[0, w].astype(F32) + g_recv[1, w].astype(F32) + g_recv[2, w].astype(F32)
        for d in (1, 2, 3):
            gz_send[w, d - 1] = g_sum[w, pl.ds(pl.multiple_of(u * lax.rem(zl + d, 4), u), u)].astype(BF)
            send(h_copy(w, d))

    over_y(0)
    with jax.named_scope("s17_onward3"):
        onward3(3)
    over_y(1)

    with jax.named_scope("s21_cwait"):

        @pl.when(x != 2 * zh + cc)
        def _():
            for n in range(4):
                arrived(zh, n)

    with jax.named_scope("s22_zwait"):
        for n in range(4):
            across(n).wait_recv()
    for n in range(4):
        cols = w_cols(n)
        own_pre = pre[:, pl.ds(pl.multiple_of(q * (2 * zh + cc) + v * lax.rem(y + 4 - FROM[n], 4), v), v)]
        both = c_in[zh, n].astype(F32) + z_in[n].astype(F32)
        gout[:, cols] = jnp.where(own_pre.astype(F32) > 0, both, 0.0).astype(BF)

    for w in (0, 1):
        with jax.named_scope("s23_hwait"):
            for d in (1, 2, 3):
                h_copy(w, d).wait_recv()
        total = g_sum[w, pl.ds(pl.multiple_of(u * zl, u), u)]
        total += gz_recv[w, 0].astype(F32) + gz_recv[w, 1].astype(F32) + gz_recv[w, 2].astype(F32)
        wout[:, w * 2 * v:(w + 1) * 2 * v] = total * scale

    for c in sent:
        c.wait_send()
    for n in range(4):
        across(n).wait_send()

    @pl.when(cc != lead)
    def _():
        own.wait_send()


def per_device(pre_act, grad_out, w_down):
    t, q = grad_out.shape
    u = w_down.shape[0]
    v = 4 * u
    half = t // 2
    vm = pltpu.VMEM
    sem = lambda *n: pltpu.SemaphoreType.DMA(n)
    space = pl.BlockSpec(memory_space=pltpu.VMEM)
    hbm = pl.BlockSpec(memory_space=pltpu.HBM)
    outs = pl.pallas_call(
        body,
        out_shape=(pltpu.VMEM((u, q), F32), pltpu.VMEM((t, q), BF)),
        in_specs=[hbm] * 3,
        out_specs=(space, space),
        scratch_shapes=[
            vm((t, pre_act.shape[1]), BF),
            vm((4 * t, q), BF), vm((4, 4 * t, v), BF), vm((4 * v, q), BF), vm((v, 4 * t), BF),
            vm((t, v), F32), vm((4, t, v), F32), vm((4, t, v), BF), vm((4, t, v), BF),
            vm((3, 4, half, v), F32), vm((3, 4, half, v), BF), vm((3, 4, half, v), BF), vm((3, 4, half, v), BF),
            vm((2, 4, t, v), BF), vm((4, t, v), BF),
            vm((3, 2, v, q // 2), BF), vm((3, 2, v, q // 2), BF), vm((2, v, q // 2), F32),
            vm((2, 3, u, q // 2), BF), vm((2, 3, u, q // 2), BF),
            sem(3), sem(3), sem(3), sem(3, 4), sem(3, 4), sem(3, 2), sem(3, 2),
            sem(3, 4), sem(3, 4), sem(3, 4), sem(3, 4),
            sem(1), sem(1), sem(3, 4), sem(3, 4), sem(3, 4), sem(2, 4, 2),
            sem(4), sem(4), sem(3, 2), sem(3, 2), sem(2, 3), sem(2, 3),
        ],
        compiler_params=pltpu.CompilerParams(
            collective_id=0, has_side_effects=True, vmem_limit_bytes=62_400_000
        ),
        name="backward",
    )(pre_act, grad_out, w_down)
    return outs[0], outs[1]


def solution(mesh):
    torus = Mesh(mesh.devices.reshape(2, mesh.shape["row"] // 2, 4, 4, 4), AXES)
    return jax.shard_map(
        per_device,
        mesh=torus,
        in_specs=(P(COL, None), P(COL, ROW), P(COL, ROW)),
        out_specs=(P(COL, ROW), P(COL, ROW)),
        check_vma=False,
    )
```

time: 518 us -> 98 us (0.19)
  waiting for transfers between devices: 478 us -> 0 us
  Pallas kernels: 0 us -> 95.7 us
  matrix products: 20.4 us -> 0 us
  between operations: 15.2 us -> 0.64 us
    reduce_scatter x4 -> x0, waiting for transfers between devices: 291 us -> none  [the longest x3 183 us: summed_rows(): subtotal = lax.psum_scatter(subtotal, axis, scatter_dimension=0, tiled=True)]
    all_gather x1 -> x0, waiting for transfers between devices: 186 us -> none  [per_device(): lax.all_gather(w_down, COL, axis=0, tiled=True)]
    pallas_call x0 -> x1, Pallas kernels: none -> 95.7 us  [per_device(): pl.pallas_call(body, out_shape=(pltpu.VMEM((u, q), F32), pltpu.VMEM((t, q...]
    dot_general x2 -> x0, matrix products: 20.4 us -> none  [the longest x1 10.3 us: per_device(): lax.dot_general(grad_out, lax.all_gather(w_down, COL, axis=0, tiled=True)...]
  transfers between devices with their start and end apart: 5 -> 0, of which waited for: 4 -> 0; matrix products, arithmetic and copies ran while one was open for 2% -> 0% of each run, Pallas kernels for 0% -> 0%
where the time goes in v2:
time: 98 us
  Pallas kernels  95.7 us (98%)
  local copies, waits for them, and re-layouts  1.58 us (2%)
    pallas_call x1, Pallas kernels, per_device(): pl.pallas_call(body, out_shape=(pltpu.VMEM((u, q), F32), pltpu.VMEM((t, q...  95.7 us

profile of v2, /device:TPU:1, one launch (start us, length us, event | category | flops | bytes accessed | tf_op | source)
XLA Modules:
  0.0 98.0 jit_solution(7236725754454622602)
XLA Ops:
  0.6 95.7 %backward.1 = (f32[64,1024]{1,0:T(8,128)S(1)}, bf16[384,1024]{1,0:T(8,128)(2,1)S(1)}) custom-call(bf16[384,4096]{1,0:T(8,128)(2,1)} %pre_h.1, bf16[384,1024]{1,0:T(8,128)(2,1)} %go_h.1, bf16[64,1024]{1,0:T(8,128)(2,1)} %wd_h.1), custom_call_target="tpu_custom_call" | custom-call | tf_op jit(solution)/shard_map/backward/pallas_call | solution.py:372
  96.4 0.7 copy.7
  97.1 0.9 copy.8

commit v3 on v2

--- a/solution.py
+++ b/solution.py
@@ -12,7 +12,14 @@
 MESH = pl.DeviceIdType.MESH
 BF = jnp.bfloat16
 F32 = jnp.float32
-TURNS = (1, 3, 2, 0)
+TURNS = (2, 1, 3, 0)
+PLAN = (
+    "p0", "z1", "w0", "z2", "w1", "z3", "b1", "b2", "c0", "w2", "w3", "c1",
+    "e0", "c2", "e1", "ar", "c3", "e2", "e3", "p1", "ow", "n0", "n1", "of",
+    "q0", "a3", "g0", "n2", "n3", "o0", "o1", "d0", "o2", "d1", "p2", "o3",
+    "d2", "p3", "d3", "q1", "g1", "r0", "r1", "q2", "g2", "r2", "q3", "g3",
+    "r3", "y0", "y1",
+)
 FROM = (0, 1, 3, 2)
 
 
@@ -125,7 +132,6 @@
             send(p_copy(slot, k))
 
     load_p.wait()
-    p_send(0)
 
     with jax.named_scope("s03_local"):
         for k in range(4):
@@ -135,26 +141,20 @@
         copy(a_half(slot, h), a_half(slot, h), a_s.at[slot - 1, h], a_r.at[slot - 1, h], dev(dx=1)).wait_recv()
 
     def a_relay():
-        a_wait(1, 0)
         send(copy(a_half(1, 0), a_half(3, 0), a_s.at[2, 0], a_r.at[2, 0], dev(dx=1)))
-        a_wait(2, 1)
         send(copy(a_half(2, 1), a_half(3, 1), a_s.at[2, 1], a_r.at[2, 1], dev(dx=3)))
 
-    for d in (1, 2, 3):
+    def w_relay(d):
+        with jax.named_scope("s05_wy"):
+            wy_wait(d % 2, d)
+            send(wy(2, d))
+
+    def w_take(d):
         with jax.named_scope("s04_wz"):
             block = w_block(0, d)
             copy(block, block, wz_s.at[d - 1], wz_r.at[d - 1], dev(dz=d)).wait_recv()
             send(wy(0, d))
             send(wy(1, d))
-        with jax.named_scope("s05_wy"):
-            wy_wait((d - 1) % 2, d - 1)
-            send(wy(2, d - 1))
-        if d == 2:
-            with jax.named_scope("s05_arelay"):
-                a_relay()
-    with jax.named_scope("s05_wy"):
-        wy_wait(1, 3)
-        send(wy(2, 3))
 
     def w_cols(n):
         return pl.ds(pl.multiple_of(v * lax.rem(y + 4 - FROM[n], 4), v), v)
@@ -193,15 +193,15 @@
 
     far = lax.rem(2 * (1 - zh) + cc + 4 - x, 4)
 
-    def onward():
-        for n in range(4):
-            arrived(1 - zh, n)
-            across(n).start()
-
-    with jax.named_scope("s06_a12"):
-        a_wait(1, 1)
-        a_wait(2, 0)
-    for n in range(4):
+    def onward(n):
+        with jax.named_scope("s10_onward1"):
+
+            @pl.when((far == 1) | (far == 3))
+            def _():
+                arrived(1 - zh, n)
+                across(n).start()
+
+    def near(n):
         with jax.named_scope("s07_wy"):
             if n in (1, 2):
                 for d in range(4):
@@ -213,71 +213,47 @@
         with jax.named_scope("s08_offer12"):
             offer(1, n)
             offer(2, n)
-            if n > 0:
-                deliver(1, n - 1)
-                deliver(2, n - 1)
-    with jax.named_scope("s08_deliver12"):
-        deliver(1, 3)
-        deliver(2, 3)
+
+    def near_out(n):
+        with jax.named_scope("s08_deliver12"):
+            deliver(1, n)
+            deliver(2, n)
 
     own = copy(o_give, o_take, o_s.at[0], o_r.at[0], dev(core=twin))
-    with jax.named_scope("s09_own"):
-        for n in range(4):
-            partial(0, n, o_keep.at[n])
-
-        @pl.when(cc != lead)
-        def _():
-            o_give[...] = o_keep[...].astype(BF)
-            own.start()
-
-    with jax.named_scope("s10_a3"):
-        a_wait(3, 0)
-        a_wait(3, 1)
-    with jax.named_scope("s10_offer3"):
-        for n in range(4):
-            offer(3, n)
-
-    with jax.named_scope("s11_own"):
-
-        @pl.when(cc == lead)
-        def _():
-            own.wait_recv()
-            c_in[lax.div(x, 2)] = (o_keep[...] + o_take[...].astype(F32)).astype(BF)
-
-            @pl.when(far == 0)
+
+    def own_part():
+        with jax.named_scope("s09_own"):
+            for n in range(4):
+                partial(0, n, o_keep.at[n])
+
+            @pl.when(cc != lead)
             def _():
-                for n in range(4):
-                    across(n).start()
-
-    def onward3(n):
-        @pl.when(far == 2)
-        def _():
-            arrived(1 - zh, n)
-            across(n).start()
-
-    with jax.named_scope("s12_deliver3"):
-        p_send(1)
-        deliver(3, 0)
-        p_send(2)
-        deliver(3, 1)
-        deliver(3, 2)
-        p_send(3)
-        deliver(3, 3)
-
-    with jax.named_scope("s13_onward1"):
-
-        @pl.when((far == 1) | (far == 3))
-        def _():
-            onward()
-
-    def g_copy(k, w):
-        return copy(g_send.at[k, w], g_recv.at[k, w], g_s.at[k, w], g_r.at[k, w], dev(dy=TURNS[k]))
-
-    def weight_part(k):
+                o_give[...] = o_keep[...].astype(BF)
+                own.start()
+
+    def own_sum():
+        with jax.named_scope("s11_own"):
+
+            @pl.when(cc == lead)
+            def _():
+                own.wait_recv()
+                c_in[lax.div(x, 2)] = (o_keep[...] + o_take[...].astype(F32)).astype(BF)
+
+                @pl.when(far == 0)
+                def _():
+                    for n in range(4):
+                        across(n).start()
+
+    def p_pass(k):
         with jax.named_scope("s14_pwait"):
             for slot in (1, 2, 3):
                 p_copy(slot, k).wait_recv()
                 send(q_copy(slot, k))
+
+    def g_copy(k, w):
+        return copy(g_send.at[k, w], g_recv.at[k, w], g_s.at[k, w], g_r.at[k, w], dev(dy=TURNS[k]))
+
+    def weight_part(k):
         with jax.named_scope("s15_qwait"):
             for slot in (1, 2, 3):
                 q_copy(slot, k).wait_recv()
@@ -299,15 +275,13 @@
                 if k < 3:
                     send(g_copy(k, w))
 
-    weight_part(0)
-    weight_part(1)
-    with jax.named_scope("s17_onward3"):
-        onward3(0)
-    weight_part(2)
-    with jax.named_scope("s17_onward3"):
-        onward3(1)
-        onward3(2)
-    weight_part(3)
+    def onward3(n):
+        with jax.named_scope("s17_onward3"):
+
+            @pl.when(far == 2)
+            def _():
+                arrived(1 - zh, n)
+                across(n).start()
 
     def h_copy(w, d):
         return copy(gz_send.at[w, d - 1], gz_recv.at[w, d - 1], h_s.at[w, d - 1], h_r.at[w, d - 1], dev(dz=d))
@@ -321,10 +295,16 @@
             gz_send[w, d - 1] = g_sum[w, pl.ds(pl.multiple_of(u * lax.rem(zl + d, 4), u), u)].astype(BF)
             send(h_copy(w, d))
 
-    over_y(0)
-    with jax.named_scope("s17_onward3"):
-        onward3(3)
-    over_y(1)
+    steps = dict(
+        z=w_take, w=w_relay, b=lambda n: (a_wait(n, 0), a_wait(n, 1)), c=near, e=near_out, p=p_send, q=p_pass, g=weight_part,
+        n=onward, r=onward3, o=lambda n: offer(3, n), d=lambda n: deliver(3, n), y=over_y,
+    )
+    single = dict(ar=a_relay, ow=own_part, of=own_sum, a3=lambda: (a_wait(3, 0), a_wait(3, 1)))
+    for step in PLAN:
+        if step in single:
+            single[step]()
+        else:
+            steps[step[0]](int(step[1]))
 
     with jax.named_scope("s21_cwait"):
 
@@ -358,6 +338,14 @@
     @pl.when(cc != lead)
     def _():
         own.wait_send()
+
+
+def store(w_v, g_v, w_h, g_h, sems):
+    copies = [pltpu.make_async_copy(w_v, w_h, sems.at[0]), pltpu.make_async_copy(g_v, g_h, sems.at[1])]
+    for c in copies:
+        c.start()
+    for c in copies:
+        c.wait()
 
 
 def per_device(pre_act, grad_out, w_down):
@@ -392,7 +380,15 @@
         ),
         name="backward",
     )(pre_act, grad_out, w_down)
-    return outs[0], outs[1]
+    return pl.pallas_call(
+        store,
+        out_shape=(jax.ShapeDtypeStruct((u, q), F32), jax.ShapeDtypeStruct((t, q), BF)),
+        in_specs=[space] * 2,
+        out_specs=(hbm, hbm),
+        scratch_shapes=[sem(2)],
+        compiler_params=pltpu.CompilerParams(vmem_limit_bytes=2**20),
+        name="store",
+    )(*outs)
 
 
 def solution(mesh):

time: 98 us -> 94.1 us (0.960)
  Pallas kernels: 95.7 us -> 93.4 us
  local copies, waits for them, and re-layouts: 1.58 us -> 0 us
    pallas_call x1, Pallas kernels: 95.7 us -> 92.4 us  [per_device(): pl.pallas_call(body, out_shape=(pltpu.VMEM((u, q), F32), pltpu.VMEM((t, q...]
    unnamed x2 -> x0, local copies, waits for them, and re-layouts: 1.58 us -> none
    pallas_call x0 -> x1, Pallas kernels: none -> 0.99 us  [per_device(): pl.pallas_call(store, out_shape=(jax.ShapeDtypeStruct((u, q), F32), jax.S...]
where the time goes in v3:
time: 94.1 us
  Pallas kernels  93.4 us (99%)
    pallas_call x1, Pallas kernels, per_device(): pl.pallas_call(body, out_shape=(pltpu.VMEM((u, q), F32), pltpu.VMEM((t, q...  92.4 us

profile of v3, /device:TPU:1, one launch (start us, length us, event | category | flops | bytes accessed | tf_op | source)
XLA Modules:
  0.0 94.1 jit_solution(1917502166797866034)
XLA Ops:
  0.6 92.4 %backward.1 = (f32[64,1024]{1,0:T(8,128)S(1)}, bf16[384,1024]{1,0:T(8,128)(2,1)S(1)}) custom-call(bf16[384,4096]{1,0:T(8,128)(2,1)} %pre_h.1, bf16[384,1024]{1,0:T(8,128)(2,1)} %go_h.1, bf16[64,1024]{1,0:T(8,128)(2,1)} %wd_h.1), custom_call_target="tpu_custom_call" | custom-call | tf_op jit(solution)/shard_map/backward/pallas_call | solution.py:360
  93.1 1.0 %store.1 = (f32[64,1024]{1,0:T(8,128)}, bf16[384,1024]{1,0:T(8,128)(2,1)}) custom-call(f32[64,1024]{1,0:T(8,128)S(1)} %get-tuple-element.4.w_v, bf16[384,1024]{1,0:T(8,128)(2,1)S(1)} %get-tuple-element.5.g_v), custom_call_target="tpu_custom_call" | custom-call | tf_op jit(solution)/shard_map/store/pallas_call | solution.py:383

commit v4 on v3

--- a/solution.py
+++ b/solution.py
@@ -18,7 +18,7 @@
     "e0", "c2", "e1", "ar", "c3", "e2", "e3", "p1", "ow", "n0", "n1", "of",
     "q0", "a3", "g0", "n2", "n3", "o0", "o1", "d0", "o2", "d1", "p2", "o3",
     "d2", "p3", "d3", "q1", "g1", "r0", "r1", "q2", "g2", "r2", "q3", "g3",
-    "r3", "y0", "y1",
+    "r3", "y0", "k0", "y1", "k1",
 )
 FROM = (0, 1, 3, 2)
 
@@ -26,9 +26,9 @@
 def body(
     pre_h, go_h, wd_h, wout, gout,
     pre, a_all, p_all, w_all, pt, acc, o_keep, o_give, o_take, keep, c_give, c_take, c_send, c_in, z_in,
-    g_send, g_recv, g_sum, gz_send, gz_recv,
+    g_send, g_recv, g_sum, gz_send, gz_recv, gz_pass,
     l_s, wz_s, wz_r, wy_s, wy_r, a_s, a_r, p_s, p_r, q_s, q_r, o_s, o_r, d_s, d_r, c_s, c_r,
-    z_s, z_r, g_s, g_r, h_s, h_r,
+    z_s, z_r, g_s, g_r, h_s, h_r, k_r,
 ):
     zh, cc, x, y, zl = [lax.axis_index(name) for name in AXES]
     t, q = go_h.shape
@@ -283,21 +283,48 @@
                 arrived(1 - zh, n)
                 across(n).start()
 
-    def h_copy(w, d):
-        return copy(gz_send.at[w, d - 1], gz_recv.at[w, d - 1], h_s.at[w, d - 1], h_r.at[w, d - 1], dev(dz=d))
+    at_end = (zl == 0) | (zl == 3)
+    inner = lax.div(zl, 3) + 1
+    end = 3 * (zl - 1)
+
+    def z_start(w, j, block, to, target, recv, more=None):
+        total = g_sum[w, pl.ds(pl.multiple_of(u * block, u), u)]
+        if more is not None:
+            total += more[...].astype(F32)
+        gz_send[w, j] = total.astype(BF)
+        copy(gz_send.at[w, j], target, h_s.at[w, j], recv, (zh, cc, x, y, to)).start()
 
     def over_y(w):
         with jax.named_scope("s20_gwait"):
             for k in range(3):
                 g_copy(k, w).wait_recv()
         g_sum[w] += g_recv[0, w].astype(F32) + g_recv[1, w].astype(F32) + g_recv[2, w].astype(F32)
-        for d in (1, 2, 3):
-            gz_send[w, d - 1] = g_sum[w, pl.ds(pl.multiple_of(u * lax.rem(zl + d, 4), u), u)].astype(BF)
-            send(h_copy(w, d))
+
+        @pl.when(at_end)
+        def _():
+            z_start(w, 0, 3 - zl, inner, gz_pass.at[w], k_r.at[w])
+            z_start(w, 2, 3 - inner, 3 - inner, gz_recv.at[w, 2], h_r.at[w, 2])
+            z_start(w, 1, inner, inner, gz_recv.at[w, 0], h_r.at[w, 0])
+
+        @pl.when(jnp.logical_not(at_end))
+        def _():
+            z_start(w, 0, 3 - zl, 3 - zl, gz_recv.at[w, 1], h_r.at[w, 1])
+            z_start(w, 1, end, end, gz_recv.at[w, 0], h_r.at[w, 0])
+
+    def z_wait(w, j):
+        copy(gz_send.at[w, j], gz_recv.at[w, j], h_s.at[w, j], h_r.at[w, j], dev(dz=1)).wait_recv()
+
+    def pass_on(w):
+        with jax.named_scope("s21_pass"):
+
+            @pl.when(jnp.logical_not(at_end))
+            def _():
+                copy(gz_send.at[w, 2], gz_pass.at[w], h_s.at[w, 2], k_r.at[w], dev(dz=1)).wait_recv()
+                z_start(w, 2, 3 - end, 3 - end, gz_recv.at[w, 1], h_r.at[w, 1], gz_pass.at[w])
 
     steps = dict(
         z=w_take, w=w_relay, b=lambda n: (a_wait(n, 0), a_wait(n, 1)), c=near, e=near_out, p=p_send, q=p_pass, g=weight_part,
-        n=onward, r=onward3, o=lambda n: offer(3, n), d=lambda n: deliver(3, n), y=over_y,
+        n=onward, r=onward3, o=lambda n: offer(3, n), d=lambda n: deliver(3, n), y=over_y, k=pass_on,
     )
     single = dict(ar=a_relay, ow=own_part, of=own_sum, a3=lambda: (a_wait(3, 0), a_wait(3, 1)))
     for step in PLAN:
@@ -324,16 +351,29 @@
 
     for w in (0, 1):
         with jax.named_scope("s23_hwait"):
-            for d in (1, 2, 3):
-                h_copy(w, d).wait_recv()
+            for j in (0, 1):
+                z_wait(w, j)
+
+        cols = pl.ds(w * 2 * v, 2 * v)
         total = g_sum[w, pl.ds(pl.multiple_of(u * zl, u), u)]
-        total += gz_recv[w, 0].astype(F32) + gz_recv[w, 1].astype(F32) + gz_recv[w, 2].astype(F32)
-        wout[:, w * 2 * v:(w + 1) * 2 * v] = total * scale
+        total += gz_recv[w, 0].astype(F32) + gz_recv[w, 1].astype(F32)
+
+        @pl.when(at_end)
+        def _():
+            wout[:, cols] = total * scale
+
+        @pl.when(jnp.logical_not(at_end))
+        def _():
+            z_wait(w, 2)
+            wout[:, cols] = (total + gz_recv[w, 2].astype(F32)) * scale
 
     for c in sent:
         c.wait_send()
     for n in range(4):
         across(n).wait_send()
+    for w in (0, 1):
+        for j in range(3):
+            copy(gz_send.at[w, j], gz_recv.at[w, j], h_s.at[w, j], h_r.at[w, j], dev(dz=1)).wait_send()
 
     @pl.when(cc != lead)
     def _():
@@ -369,11 +409,11 @@
             vm((3, 4, half, v), F32), vm((3, 4, half, v), BF), vm((3, 4, half, v), BF), vm((3, 4, half, v), BF),
             vm((2, 4, t, v), BF), vm((4, t, v), BF),
             vm((3, 2, v, q // 2), BF), vm((3, 2, v, q // 2), BF), vm((2, v, q // 2), F32),
-            vm((2, 3, u, q // 2), BF), vm((2, 3, u, q // 2), BF),
+            vm((2, 3, u, q // 2), BF), vm((2, 3, u, q // 2), BF), vm((2, u, q // 2), BF),
             sem(3), sem(3), sem(3), sem(3, 4), sem(3, 4), sem(3, 2), sem(3, 2),
             sem(3, 4), sem(3, 4), sem(3, 4), sem(3, 4),
             sem(1), sem(1), sem(3, 4), sem(3, 4), sem(3, 4), sem(2, 4, 2),
-            sem(4), sem(4), sem(3, 2), sem(3, 2), sem(2, 3), sem(2, 3),
+            sem(4), sem(4), sem(3, 2), sem(3, 2), sem(2, 3), sem(2, 3), sem(2),
         ],
         compiler_params=pltpu.CompilerParams(
             collective_id=0, has_side_effects=True, vmem_limit_bytes=62_400_000

time: 94.1 us -> 93.1 us (0.989)
  Pallas kernels: 93.4 us -> 91.9 us
    pallas_call x1, Pallas kernels: 92.4 us -> 90.9 us  [per_device(): pl.pallas_call(body, out_shape=(pltpu.VMEM((u, q), F32), pltpu.VMEM((t, q...]
where the time goes in v4:
time: 93.1 us; the launch traced here: 92.6 us
  Pallas kernels  91.9 us (99%)
    pallas_call x1, Pallas kernels, per_device(): pl.pallas_call(body, out_shape=(pltpu.VMEM((u, q), F32), pltpu.VMEM((t, q...  90.9 us

profile of v4, /device:TPU:1, one launch (start us, length us, event | category | flops | bytes accessed | tf_op | source)
XLA Modules:
  0.0 92.6 jit_solution(6755018804214242253)
XLA Ops:
  0.6 90.9 %backward.1 = (f32[64,1024]{1,0:T(8,128)S(1)}, bf16[384,1024]{1,0:T(8,128)(2,1)S(1)}) custom-call(bf16[384,4096]{1,0:T(8,128)(2,1)} %pre_h.1, bf16[384,1024]{1,0:T(8,128)(2,1)} %go_h.1, bf16[64,1024]{1,0:T(8,128)(2,1)} %wd_h.1), custom_call_target="tpu_custom_call" | custom-call | tf_op jit(solution)/shard_map/backward/pallas_call | solution.py:400
  91.6 1.0 %store.1 = (f32[64,1024]{1,0:T(8,128)}, bf16[384,1024]{1,0:T(8,128)(2,1)}) custom-call(f32[64,1024]{1,0:T(8,128)S(1)} %get-tuple-element.4.w_v, bf16[384,1024]{1,0:T(8,128)(2,1)S(1)} %get-tuple-element.5.g_v), custom_call_target="tpu_custom_call" | custom-call | tf_op jit(solution)/shard_map/store/pallas_call | solution.py:423

commit v5 on v4

--- a/solution.py
+++ b/solution.py
@@ -16,9 +16,9 @@
 PLAN = (
     "p0", "z1", "w0", "z2", "w1", "z3", "b1", "b2", "c0", "w2", "w3", "c1",
     "e0", "c2", "e1", "ar", "c3", "e2", "e3", "p1", "ow", "n0", "n1", "of",
-    "q0", "a3", "g0", "n2", "n3", "o0", "o1", "d0", "o2", "d1", "p2", "o3",
-    "d2", "p3", "d3", "q1", "g1", "r0", "r1", "q2", "g2", "r2", "q3", "g3",
-    "r3", "y0", "k0", "y1", "k1",
+    "q0", "a3", "g0", "n2", "n3", "o0", "o1", "d0", "d1", "p2", "o2", "o3",
+    "d2", "d3", "p3", "q1", "g1", "r0", "r1", "q2", "g2", "r2", "r3", "q3",
+    "g3", "y0", "k0", "y1", "k1",
 )
 FROM = (0, 1, 3, 2)
 

time: 93.1 us -> 92.6 us (level)
  no operation moved by 1% of the time
where the time goes in v5:
time: 92.6 us; the launch traced here: 92.5 us
  Pallas kernels  91.9 us (99%)
    pallas_call x1, Pallas kernels, per_device(): pl.pallas_call(body, out_shape=(pltpu.VMEM((u, q), F32), pltpu.VMEM((t, q...  90.9 us

profile of v5, /device:TPU:1, one launch (start us, length us, event | category | flops | bytes accessed | tf_op | source)
XLA Modules:
  0.0 92.5 jit_solution(10887217943057094997)
XLA Ops:
  0.6 90.9 %backward.1 = (f32[64,1024]{1,0:T(8,128)S(1)}, bf16[384,1024]{1,0:T(8,128)(2,1)S(1)}) custom-call(bf16[384,4096]{1,0:T(8,128)(2,1)} %pre_h.1, bf16[384,1024]{1,0:T(8,128)(2,1)} %go_h.1, bf16[64,1024]{1,0:T(8,128)(2,1)} %wd_h.1), custom_call_target="tpu_custom_call" | custom-call | tf_op jit(solution)/shard_map/backward/pallas_call | solution.py:400
  91.5 1.0 %store.1 = (f32[64,1024]{1,0:T(8,128)}, bf16[384,1024]{1,0:T(8,128)(2,1)}) custom-call(f32[64,1024]{1,0:T(8,128)S(1)} %get-tuple-element.4.w_v, bf16[384,1024]{1,0:T(8,128)(2,1)S(1)} %get-tuple-element.5.g_v), custom_call_target="tpu_custom_call" | custom-call | tf_op jit(solution)/shard_map/store/pallas_call | solution.py:423
